TPU v7x, 256 devices: a whole 4x4x8 slice. The times are simulated.
256 devices in a mesh: vocab: 64 (over x, z, core), seq: 4 (over y).
Axes of the slice: x: 4, y: 4, z: 8, core: 2. Of those that a mesh axis runs over, the one named last changes fastest.
Arguments:
- hidden: bfloat16 [4096, 4096], P(('vocab', 'seq')), may hold values from -40 to 40
- embedding: bfloat16 [65536, 4096], P('vocab'), may hold values from -40 to 40
- logit_scale: float32 [65536], P('vocab'), may hold values from 100 to 600
- targets: int32 [4096], P(('vocab', 'seq')), may hold values from 0 to 65535
Outputs:
- token_loss: float32 [4096], P(('vocab', 'seq'))
- mean_loss: float32 [], replicated
All inputs are finite; a program needn't handle non-finite values.
Results may differ from a plain program's by a relative error of at most 0.0012.
Values may be sent and summed in bfloat16 or wider, within the bound.
No kernel may reach another device: no remote copies, remote signals or barrier semaphores. Data moves between devices by JAX's collectives and lax.ppermute only.
A program may use at most 64 MiB of HBM per device.

v0:
```python
import functools

import jax
import jax.numpy as jnp
from jax import lax
from jax.experimental import pallas as pl
from jax.experimental.pallas import tpu as pltpu
from jax.sharding import PartitionSpec as P


epsilon = 1e-06
NX, NZ, NC, NY = 4, 8, 2, 4
D = 4096
CA = 1024
CB = D - CA
CT = 128
ROWS = 16
HALF = NZ * ROWS
BLOCK = 512
f32, bf16 = jnp.float32, jnp.bfloat16
VMEM = pl.BlockSpec(memory_space=pltpu.VMEM)


def index_of(x, z, core):
    return ((x % NX) * NZ + z % NZ) * NC + core


def shift(array, dx, dz, flip=0):
    pairs = [
        (index_of(x, z, c), index_of(x + dx, z + dz, c ^ flip))
        for x in range(NX)
        for z in range(NZ)
        for c in range(NC)
    ]
    return lax.ppermute(array, "vocab", pairs)


def call(kernel, out_shape, limit, scratch=(), cost=None, specs=None):
    return lambda *args: pl.pallas_call(
        kernel,
        out_shape=out_shape,
        in_specs=specs or [VMEM] * len(args),
        out_specs=jax.tree.map(lambda _: VMEM, out_shape),
        scratch_shapes=list(scratch),
        compiler_params=pltpu.CompilerParams(vmem_limit_bytes=limit),
        cost_estimate=cost,
    )(*args)


def unit_kernel(
    hidden_hbm, target_hbm, scale_hbm, unit_ref, a_ref, b_ref, scale_ref, hidden_ref, target_ref, arrived
):
    copies = (
        pltpu.make_async_copy(scale_hbm, scale_ref, arrived.at[2]),
        pltpu.make_async_copy(hidden_hbm, hidden_ref, arrived.at[0]),
        pltpu.make_async_copy(target_hbm, target_ref, arrived.at[1]),
    )
    for copy in copies:
        copy.start()
    for copy in copies:
        copy.wait()
    wide = hidden_ref[...].astype(f32)
    unit = wide * lax.rsqrt(jnp.sum(wide * wide, axis=1, keepdims=True) + epsilon)
    unit = unit.astype(bf16)
    row = lax.broadcasted_iota(jnp.int32, (ROWS, ROWS), 0)
    column = lax.broadcasted_iota(jnp.int32, (ROWS, ROWS), 1)
    target = jnp.where(row == column, jnp.broadcast_to(target_ref[...], (ROWS, ROWS)), 0)
    high = jnp.sum((target // 256).astype(f32), axis=1, keepdims=True)
    low = jnp.sum((target % 256).astype(f32), axis=1, keepdims=True)
    lane = lax.broadcasted_iota(jnp.int32, (ROWS, CT), 1)
    coded = jnp.where(lane == 0, high, jnp.where(lane == 1, low, 0.0)).astype(bf16)
    unit_ref[:, :D] = unit
    unit_ref[:, D:] = coded
    a_ref[...] = unit[:, :CA]
    b_ref[:, :CB] = unit[:, CA:]
    b_ref[:, CB:] = coded


def place(index):
    core = index % NC
    z = (index // NC) % NZ
    return index // (NC * NZ), z, core


def head_kernel(a_spots, b_spots, last, counts, *refs):
    n_a, n_b = counts
    if last:
        tables, gains, first_ref, *rest = refs
    else:
        own_ref, swapped_ref, own_scale, swapped_scale, *rest = refs
    a_refs, b_refs, rest = rest[:n_a], rest[n_a : n_a + n_b], rest[n_a + n_b :]
    if last:
        out_ref, tokens, coded, logits = rest
    else:
        out_ref, tables, gains, tokens, coded, logits, scales, arrived = rest
    rows = tables.shape[0] // 2
    blocks = 2 * rows // BLOCK

    if not last:
        for k in range(blocks):
            source = (own_ref, swapped_ref)[k * BLOCK // rows]
            at = pl.ds(k * BLOCK % rows, BLOCK)
            pltpu.make_async_copy(
                source.at[at], tables.at[pl.ds(k * BLOCK, BLOCK)], arrived.at[k]
            ).start()
        scales[: rows // 128, :] = own_scale[...]
        scales[rows // 128 :, :] = swapped_scale[...]
    index = lax.axis_index("vocab")
    x, z, core = place(index)

    def spot(half, dz):
        return pl.ds(pl.multiple_of(half * HALF + lax.rem(z + dz + NZ, NZ) * ROWS, ROWS), ROWS)

    for buffer, row, column, half, dz in a_spots:
        tokens[spot(half, dz), :CA] = a_refs[buffer][row : row + ROWS, column : column + CA]
    for buffer, row, column, half, dz in b_spots:
        ref = b_refs[buffer]
        tokens[spot(half, dz), CA:] = ref[row : row + ROWS, column : column + CB]
        coded[spot(half, dz), :] = ref[row : row + ROWS, column + CB : column + CB + CT].astype(f32)
    code = coded[...].T
    target = (code[0:1, :] * 256.0 + code[1:2, :]).astype(jnp.int32)
    own_base, swapped_base = index * rows, (index - 2 * core) * rows

    def step(k, carry):
        peak, picked = carry
        part = pl.ds(pl.multiple_of(k * BLOCK, BLOCK), BLOCK)
        if not last:
            pltpu.make_async_copy(own_ref.at[pl.ds(0, BLOCK)], tables.at[part], arrived.at[k]).wait()
            for j in range(BLOCK // 128):
                some = pl.ds(pl.multiple_of(k * BLOCK + j * 128, 128), 128)
                total = jnp.zeros((128, 128), f32)
                for i in range(D // 128):
                    piece = tables[some, i * 128 : (i + 1) * 128].astype(f32)
                    total += piece * piece
                norm = lax.rsqrt(jnp.sum(total, axis=1, keepdims=True) + epsilon)
                scale = scales[pl.ds(k * (BLOCK // 128) + j, 1), :]
                gains[some, :] = norm * jnp.broadcast_to(scale, (128, 128)).T
        value = lax.dot_general(
            tables[part, :], tokens[...], (((1,), (1,)), ((), ())), preferred_element_type=f32
        )
        factor = gains[part, :]
        value = value * jnp.concatenate([factor, factor], axis=1)
        logits[part, :] = value
        base = jnp.where(k * BLOCK < rows, own_base, swapped_base) + k * BLOCK
        row = lax.broadcasted_iota(jnp.int32, (BLOCK, 256), 0)
        chosen = jnp.where(row == target - base, value, 0.0)
        peak = jnp.maximum(peak, jnp.max(value.reshape(BLOCK // 8, 8, 256), axis=0))
        picked = picked + jnp.sum(chosen.reshape(BLOCK // 8, 8, 256), axis=0)
        return peak, picked

    peak, picked = lax.fori_loop(
        0, blocks, step, (jnp.full((8, 256), -jnp.inf, f32), jnp.zeros((8, 256), f32))
    )
    peak = jnp.max(peak, axis=0, keepdims=True)

    def add(k, total):
        part = pl.ds(pl.multiple_of(k * 256, 256), 256)
        term = jnp.exp(logits[part, :] - peak)
        return total + jnp.sum(term.reshape(32, 8, 256), axis=0)

    total = lax.fori_loop(0, 2 * rows // 256, add, jnp.zeros((8, 256), f32))
    log_sum = peak + jnp.log(jnp.sum(total, axis=0, keepdims=True))
    picked = jnp.sum(picked, axis=0, keepdims=True)
    row = lax.broadcasted_iota(jnp.int32, (8, 128), 0)
    both = first_ref[...] if last else jnp.zeros((8, 128), f32)
    for half, dx in enumerate((0, 2) if last else (-1, 1)):
        xs = lax.rem(x + dx + NX, NX)
        lanes = slice(half * 128, half * 128 + 128)
        both = jnp.where(row == xs, log_sum[:, lanes], both)
        both = jnp.where(row == xs + NX, picked[:, lanes], both)
    out_ref[...] = jnp.broadcast_to(both[None], out_ref.shape) if last else both


def close_kernel(pieces_ref, loss_ref, sum_ref):
    log_sum = pieces_ref[:, :NX, :]
    peak = jnp.max(log_sum, axis=0)
    total = jnp.sum(jnp.exp(log_sum - peak[None]), axis=0)
    loss = peak + jnp.log(total) - jnp.sum(pieces_ref[:, NX:, :], axis=0)
    loss_ref[...] = loss
    summed = jnp.sum(jnp.sum(loss, axis=0, keepdims=True), axis=1, keepdims=True)
    sum_ref[...] = jnp.broadcast_to(summed[None], sum_ref.shape)


def head_loss(hidden, embedding, logit_scale, targets):
    rows = embedding.shape[0]
    index = lax.axis_index("vocab")
    x, z, _ = place(index)
    swapped = shift(embedding, 0, 0, 1)
    any_space = pl.BlockSpec(memory_space=pltpu.HBM)
    unit, a, b, own_scale = call(
        unit_kernel,
        (
            pltpu.VMEM((ROWS, D + CT), bf16),
            pltpu.VMEM((ROWS, CA), bf16),
            pltpu.VMEM((ROWS, CB + CT), bf16),
            pltpu.VMEM((rows // 128, 128), f32),
        ),
        58 << 20,
        (
            pltpu.VMEM((ROWS, D), bf16),
            pltpu.VMEM((1, ROWS), jnp.int32),
            pltpu.SemaphoreType.DMA((3,)),
        ),
        specs=[any_space] * 3,
    )(hidden, targets.reshape(1, ROWS), logit_scale.reshape(rows // 128, 128))
    swapped_scale = shift(own_scale, 0, 0, 1)

    a_far = shift(a, 2, 0)
    left, right = shift(unit, 1, 0), shift(unit, -1, 0)
    b1, c1, b2, c2 = shift(b, 0, 1), shift(b, 0, -1), shift(b, 0, 2), shift(b, 0, -2)
    line = jnp.concatenate([left[:, :CA], right[:, :CA], a, a_far])
    p1, m1 = shift(line, 0, 1), shift(line, 0, -1)
    near = jnp.concatenate([b1, c1, b2, c2])
    q1, n1 = shift(near, 1, 0), shift(near, -1, 0)
    p2, m2 = shift(line, 0, 2), shift(line, 0, -2)
    b3, c3, b4 = shift(b2, 0, 1), shift(c2, 0, -1), shift(b2, 0, 2)
    p3, m3, p4 = shift(p2, 0, 1), shift(m2, 0, -1), shift(p2, 0, 2)
    apart = jnp.concatenate([b3, c3, b4])
    q2, n2 = shift(apart, 1, 0), shift(apart, -1, 0)
    q3 = shift(q1, 1, 0)
    n3 = shift(jnp.concatenate([right[:, CA:], n2]), -1, 0)

    lines = (line, p1, m1, p2, m2, p3, m3, p4)
    line_dz = (0, -1, 1, -2, 2, -3, 3, -4)
    near_dz, apart_dz = (-1, 1, -2, 2), (-3, 3, -4)

    def spots(buffer, half, offsets, column=0):
        return [(buffer, k * ROWS, column, half, dz) for k, dz in enumerate(offsets)]

    cost = pl.CostEstimate(
        flops=2 * 2 * rows * D * 256, bytes_accessed=16 * rows * D, transcendentals=0
    )
    scratch = (
        pltpu.VMEM((256, D), bf16),
        pltpu.VMEM((256, CT), f32),
        pltpu.VMEM((2 * rows, 256), f32),
    )

    def head(a_spots, b_spots, given, specs, sources, name):
        last = name == "head_column"
        piece = jax.ShapeDtypeStruct((NX * NZ, 8, 128) if last else (8, 128), f32)
        kept = (pltpu.VMEM((2 * rows, D), bf16), pltpu.VMEM((2 * rows, 128), f32))
        more = (
            pltpu.VMEM((2 * rows // 128, 128), f32),
            pltpu.SemaphoreType.DMA((2 * rows // BLOCK,)),
        )
        return call(
            functools.partial(head_kernel, a_spots, b_spots, last, (len(lines), len(sources))),
            piece if last else (piece, *kept),
            28 << 20,
            scratch if last else scratch + more,
            cost,
            specs + [VMEM] * (len(lines) + len(sources)),
        )(*given, *lines, *sources)

    a_spots = [(k, half * ROWS, 0, half, dz) for k, dz in enumerate(line_dz) for half in (0, 1)]
    b_spots = []
    for half in (0, 1):
        b_spots += spots(3 * half, half, (0,), CA)
        b_spots += spots(3 * half + 1, half, near_dz)
        b_spots += spots(3 * half + 2, half, apart_dz)
    sides = (left, q1, q2, right, n1, n2)
    given = (embedding, swapped, own_scale, swapped_scale)
    specs = [any_space] * 2 + [VMEM] * 2
    first, tables, gains = head(a_spots, b_spots, given, specs, sides, "head_sides")
    a_spots = [
        (k, (2 + half) * ROWS, 0, half, dz) for k, dz in enumerate(line_dz) for half in (0, 1)
    ]
    b_spots = spots(0, 0, (0,)) + spots(1, 0, near_dz) + spots(2, 0, apart_dz)
    b_spots += spots(3, 1, near_dz) + spots(4, 1, (0,) + apart_dz)
    columns = (b, near, apart, q3, n3)
    given = (tables, gains, first)
    pieces = head(a_spots, b_spots, given, [VMEM] * 3, columns, "head_column")

    same_core = [[v for v in range(NX * NZ * NC) if v % NC == c] for c in range(NC)]
    pieces = lax.all_to_all(pieces, "vocab", 0, 0, tiled=True, axis_index_groups=same_core)
    loss, summed = call(
        close_kernel,
        (jax.ShapeDtypeStruct((NX, 128), f32), jax.ShapeDtypeStruct((NY * NC, 1, 128), f32)),
        4 << 20,
    )(pieces)
    groups = [
        [(v + c) * NY + s for c in range(NC) for s in range(NY)]
        for v in range(0, NX * NZ * NC, NC)
    ]
    summed = lax.all_to_all(summed, ("vocab", "seq"), 0, 0, tiled=True, axis_index_groups=groups)
    mean_loss = jnp.sum(summed[:, 0, 0]) / (NX * NZ * NC * NY * ROWS)
    own_loss = lax.dynamic_slice(loss, (x, z * ROWS), (1, ROWS)).reshape(ROWS)
    return own_loss, mean_loss


def solution(mesh):
    in_specs = (P(("vocab", "seq"), None), P("vocab", None), P("vocab"), P(("vocab", "seq")))
    out_specs = (P(("vocab", "seq")), P())
    return jax.shard_map(
        head_loss, mesh=mesh, in_specs=in_specs, out_specs=out_specs, check_vma=False
    )
```

profile of v0, /device:TPU:1, one launch (start us, length us, event | category | flops | bytes accessed | tf_op | source)
XLA Modules:
  0.0 108.2 jit_solution(14240866277390495152)
XLA Ops:
  0.6 3.3 %collective-permute-start = (bf16[1024,4096]{1,0:T(8,128)(2,1)}, bf16[1024,4096]{1,0:T(8,128)(2,1)}, u32[]{:S(2)}, u32[]{:S(2)}) collective-permute-start(bf16[1024,4096]{1,0:T(8,128)(2,1)} %refs_0_.1), channel_id=1, source_target_pairs={{0,4},{4,0},{8,12},{12,8},{16,20},{20,16},{24,28},{28,24},{32,36},... | collective-permute-start | bytes 25165832 | tf_op jit(solution)/shard_map/ppermute | solution.py:35
  3.9 1.1 %shard_map.59 = (bf16[16,4224]{1,0:T(8,128)(2,1)S(1)}, bf16[16,1024]{1,0:T(8,128)(2,1)S(1)}, bf16[16,3200]{1,0:T(8,128)(2,1)S(1)}, f32[8,128]{1,0:T(8,128)S(1)}) custom-call(bf16[16,4096]{1,0:T(8,128)(2,1)} %hidden_hbm.1, s32[1,16]{1,0:T(1,128)} %bitcast.5, f32[8,128]{1,0:T(8,128)} %bitcast.4), custom_call_target="tpu_custom_call" | custom-call | tf_op jit(solution)/shard_map/pallas_call | solution.py:39
  5.1 3.9 %collective-permute-start.13 = (bf16[16,3200]{1,0:T(8,128)(2,1)S(1)}, bf16[16,3200]{1,0:T(8,128)(2,1)S(1)}, u32[]{:S(2)}, u32[]{:S(2)}) collective-permute-start(bf16[16,3200]{1,0:T(8,128)(2,1)S(1)} %get-tuple-element.14.refs_11_), channel_id=1, source_target_pairs={{0,56},{4,60},{8,0},{12,4},{16,8},{20,12},{24,16},{28,20},{32,24},... | collective-permute-start | bytes 307208 | tf_op jit(solution)/shard_map/ppermute | solution.py:35
  9.1 3.6 %collective-permute-start.15 = (bf16[16,3200]{1,0:T(8,128)(2,1)S(1)}, bf16[16,3200]{1,0:T(8,128)(2,1)S(1)}, u32[]{:S(2)}, u32[]{:S(2)}) collective-permute-start(bf16[16,3200]{1,0:T(8,128)(2,1)S(1)} %get-tuple-element.14.refs_11_), channel_id=1, source_target_pairs={{0,48},{4,52},{8,56},{12,60},{16,0},{20,4},{24,8},{28,12},{32,16},... | collective-permute-start | bytes 307208 | tf_op jit(solution)/shard_map/ppermute | solution.py:35
  12.6 2.5 %collective-permute-start.3 = (bf16[16,4224]{1,0:T(8,128)(2,1)S(1)}, bf16[16,4224]{1,0:T(8,128)(2,1)S(1)}, u32[]{:S(2)}, u32[]{:S(2)}) collective-permute-start(bf16[16,4224]{1,0:T(8,128)(2,1)S(1)} %get-tuple-element.12), channel_id=1, source_target_pairs={{0,192},{4,196},{8,200},{12,204},{16,208},{20,212},{24,216},{28,22... | collective-permute-start | bytes 405512 | tf_op jit(solution)/shard_map/ppermute | solution.py:35
  15.2 1.0 collective-permute-done.14
  16.3 2.7 %collective-permute-start.4 = (bf16[16,1024]{1,0:T(8,128)(2,1)S(1)}, bf16[16,1024]{1,0:T(8,128)(2,1)S(1)}, u32[]{:S(2)}, u32[]{:S(2)}) collective-permute-start(bf16[16,1024]{1,0:T(8,128)(2,1)S(1)} %get-tuple-element.13), channel_id=1, source_target_pairs={{0,128},{4,132},{8,136},{12,140},{16,144},{20,148},{24,152},{28,15... | collective-permute-start | bytes 98312 | tf_op jit(solution)/shard_map/ppermute | solution.py:35
  19.0 2.7 %collective-permute-start.1 = (f32[8,128]{1,0:T(8,128)S(1)}, f32[8,128]{1,0:T(8,128)S(1)}, u32[]{:S(2)}, u32[]{:S(2)}) collective-permute-start(f32[8,128]{1,0:T(8,128)S(1)} %get-tuple-element.11.refs_2_), channel_id=1, source_target_pairs={{0,4},{4,0},{8,12},{12,8},{16,20},{20,16},{24,28},{28,24},{32,36},... | collective-permute-start | bytes 12296 | tf_op jit(solution)/shard_map/ppermute | solution.py:35
  22.2 2.3 %collective-permute-start.18 = (bf16[16,3200]{1,0:T(8,128)(2,1)S(1)}, bf16[16,3200]{1,0:T(8,128)(2,1)S(1)}, u32[]{:S(2)}, u32[]{:S(2)}) collective-permute-start(bf16[16,3200]{1,0:T(8,128)(2,1)S(1)} %collective-permute-done.15), channel_id=1, source_target_pairs={{0,56},{4,60},{8,0},{12,4},{16,8},{20,12},{24,16},{28,20},{32,24},... | collective-permute-start | bytes 307208 | tf_op jit(solution)/shard_map/ppermute | solution.py:35
  24.5 2.0 %collective-permute-done.17 = bf16[16,3200]{1,0:T(8,128)(2,1)S(1)} collective-permute-done((bf16[16,3200]{1,0:T(8,128)(2,1)S(1)}, bf16[16,3200]{1,0:T(8,128)(2,1)S(1)}, u32[]{:S(2)}, u32[]{:S(2)}) %collective-permute-start.17) | collective-permute-done | bytes 102432 | tf_op jit(solution)/shard_map/ppermute | solution.py:35
  26.5 0.8 collective-permute-start.7
  27.4 1.0 collective-permute-done.18
  28.4 1.8 %collective-permute-start.8 = (bf16[64,1024]{1,0:T(8,128)(2,1)S(1)}, bf16[64,1024]{1,0:T(8,128)(2,1)S(1)}, u32[]{:S(2)}, u32[]{:S(2)}) collective-permute-start(bf16[64,1024]{1,0:T(8,128)(2,1)S(1)} %pad_maximum_fusion.1.refs_4_.refs_3_), channel_id=1, source_target_pairs={{0,48},{4,52},{8,56},{12,60},{16,0},{20,4},{24,8},{28,12},{32,16},... | collective-permute-start | bytes 393224 | tf_op jit(solution)/shard_map/ppermute | solution.py:35
  30.2 0.8 collective-permute-start.5
  31.1 2.0 %collective-permute-start.6 = (bf16[64,1024]{1,0:T(8,128)(2,1)S(1)}, bf16[64,1024]{1,0:T(8,128)(2,1)S(1)}, u32[]{:S(2)}, u32[]{:S(2)}) collective-permute-start(bf16[64,1024]{1,0:T(8,128)(2,1)S(1)} %pad_maximum_fusion.1.refs_4_.refs_3_), channel_id=1, source_target_pairs={{0,56},{4,60},{8,0},{12,4},{16,8},{20,12},{24,16},{28,20},{32,24},... | collective-permute-start | bytes 393224 | tf_op jit(solution)/shard_map/ppermute | solution.py:35
  33.5 4.7 %collective-permute-start.22 = (bf16[48,3200]{1,0:T(8,128)(2,1)S(1)}, bf16[48,3200]{1,0:T(8,128)(2,1)S(1)}, u32[]{:S(2)}, u32[]{:S(2)}) collective-permute-start(bf16[48,3200]{1,0:T(8,128)(2,1)S(1)} %constant_dynamic-update-slice_fusion.4.refs_13_), channel_id=1, source_target_pairs={{0,192},{4,196},{8,200},{12,204},{16,208},{20,212},{24,216},{28,22... | collective-permute-start | bytes 921608 | tf_op jit(solution)/shard_map/ppermute | solution.py:35
  38.2 1.0 collective-permute-start.11
  39.5 1.7 %collective-permute-start.16 = (bf16[64,3200]{1,0:T(8,128)(2,1)S(1)}, bf16[64,3200]{1,0:T(8,128)(2,1)S(1)}, u32[]{:S(2)}, u32[]{:S(2)}) collective-permute-start(bf16[64,3200]{1,0:T(8,128)(2,1)S(1)} %constant_dynamic-update-slice_fusion.refs_12_), channel_id=1, source_target_pairs={{0,64},{4,68},{8,72},{12,76},{16,80},{20,84},{24,88},{28,92},{32,9... | collective-permute-start | bytes 1228808 | tf_op jit(solution)/shard_map/ppermute | solution.py:35
  41.2 4.6 %collective-permute-done.11.refs_11_.refs_10_ = bf16[64,1024]{1,0:T(8,128)(2,1)S(1)} collective-permute-done((bf16[64,1024]{1,0:T(8,128)(2,1)S(1)}, bf16[64,1024]{1,0:T(8,128)(2,1)S(1)}, u32[]{:S(2)}, u32[]{:S(2)}) %collective-permute-start.11) | collective-permute-done | bytes 131104 | tf_op jit(solution)/shard_map/ppermute | solution.py:35
  46.2 1.1 collective-permute-start.20
  47.2 2.1 %collective-permute-start.10 = (bf16[64,1024]{1,0:T(8,128)(2,1)S(1)}, bf16[64,1024]{1,0:T(8,128)(2,1)S(1)}, u32[]{:S(2)}, u32[]{:S(2)}) collective-permute-start(bf16[64,1024]{1,0:T(8,128)(2,1)S(1)} %collective-permute-done.8.refs_8_.refs_7_), channel_id=1, source_target_pairs={{0,56},{4,60},{8,0},{12,4},{16,8},{20,12},{24,16},{28,20},{32,24},... | collective-permute-start | bytes 393224 | tf_op jit(solution)/shard_map/ppermute | solution.py:35
  49.4 1.9 %collective-permute-done.10.refs_10_.refs_9_ = bf16[64,1024]{1,0:T(8,128)(2,1)S(1)} collective-permute-done((bf16[64,1024]{1,0:T(8,128)(2,1)S(1)}, bf16[64,1024]{1,0:T(8,128)(2,1)S(1)}, u32[]{:S(2)}, u32[]{:S(2)}) %collective-permute-start.10) | collective-permute-done | bytes 131104 | tf_op jit(solution)/shard_map/ppermute | solution.py:35
  51.4 2.6 %collective-permute-start.24 = (bf16[64,3200]{1,0:T(8,128)(2,1)S(1)}, bf16[64,3200]{1,0:T(8,128)(2,1)S(1)}, u32[]{:S(2)}, u32[]{:S(2)}) collective-permute-start(bf16[64,3200]{1,0:T(8,128)(2,1)S(1)} %pad_maximum_fusion), channel_id=1, source_target_pairs={{0,192},{4,196},{8,200},{12,204},{16,208},{20,212},{24,216},{28,22... | collective-permute-start | bytes 1228808 | tf_op jit(solution)/shard_map/ppermute | solution.py:35
  54.0 2.7 %collective-permute-done.20.refs_14_ = bf16[48,3200]{1,0:T(8,128)(2,1)S(1)} collective-permute-done((bf16[48,3200]{1,0:T(8,128)(2,1)S(1)}, bf16[48,3200]{1,0:T(8,128)(2,1)S(1)}, u32[]{:S(2)}, u32[]{:S(2)}) %collective-permute-start.20) | collective-permute-done | bytes 307232 | tf_op jit(solution)/shard_map/ppermute | solution.py:35
  56.7 10.6 %shard_map.60 = (f32[8,128]{1,0:T(8,128)S(1)}, bf16[2048,4096]{1,0:T(8,128)(2,1)S(1)}, f32[2048,128]{1,0:T(8,128)S(1)}) custom-call(bf16[1024,4096]{1,0:T(8,128)(2,1)} %refs_0_.1, bf16[1024,4096]{1,0:T(8,128)(2,1)} %collective-permute-done.refs_1_, f32[8,128]{1,0:T(8,128)S(1)} %get-tuple-element.11.refs_2_, f32[8,128]{1,0:T(8,128)S(1)} %collective-permute-done.1.refs_3_, ...), custom_call_target="tpu_custom_call" | custom-call | flops 4294967296 | bytes 67108864 | tf_op jit(solution)/shard_map/pallas_call | solution.py:39
  67.4 6.6 %shard_map.61 = f32[32,8,128]{2,1,0:T(8,128)} custom-call(bf16[2048,4096]{1,0:T(8,128)(2,1)S(1)} %get-tuple-element.15.refs_0_, f32[2048,128]{1,0:T(8,128)S(1)} %get-tuple-element.16.refs_1_, f32[8,128]{1,0:T(8,128)S(1)} %get-tuple-element.17.refs_2_, bf16[64,1024]{1,0:T(8,128)(2,1)S(1)} %pad_maximum_fusion.1.refs_4_.refs_3_, ...), custom_call_target="tpu_custom_call" | custom-call | flops 4294967296 | bytes 67108864 | tf_op jit(solution)/shard_map/pallas_call | solution.py:39
  74.0 7.7 %all-to-all-start = ((f32[32,8,128]{2,1,0:T(8,128)}), f32[32,8,128]{2,1,0:T(8,128)S(1)}, u32[]{:S(2)}, u32[]{:S(2)}) async-start(f32[32,8,128]{2,1,0:T(8,128)} %shard_map.61), calls=%async_computation | async-start | bytes 262144 | tf_op jit(solution)/shard_map/all_to_all | solution.py:276
  81.8 9.1 %all-to-all-done.pieces_ref = f32[32,8,128]{2,1,0:T(8,128)S(1)} async-done(((f32[32,8,128]{2,1,0:T(8,128)}), f32[32,8,128]{2,1,0:T(8,128)S(1)}, u32[]{:S(2)}, u32[]{:S(2)}) %all-to-all-start) | async-done | bytes 131104 | tf_op jit(solution)/shard_map/all_to_all | solution.py:276
  90.9 0.7 shard_map.62
  91.6 9.6 %all-to-all-start.1 = ((f32[8,1,128]{2,1,0:T(1,128)}), f32[8,1,128]{2,1,0:T(1,128)S(1)}, u32[]{:S(2)}, u32[]{:S(2)}) async-start(f32[8,1,128]{2,1,0:T(1,128)} %get-tuple-element.19), calls=%async_computation.1 | async-start | bytes 8192 | tf_op jit(solution)/shard_map/all_to_all | solution.py:286
  101.8 4.0 %all-to-all-done.1 = f32[8,1,128]{2,1,0:T(1,128)S(1)} async-done(((f32[8,1,128]{2,1,0:T(1,128)}), f32[8,1,128]{2,1,0:T(1,128)S(1)}, u32[]{:S(2)}, u32[]{:S(2)}) %all-to-all-start.1) | async-done | bytes 4128 | tf_op jit(solution)/shard_map/all_to_all | solution.py:286
  105.9 0.6 slice_reduce_fusion
  (40 shorter events, 2.5 us)
Async XLA Ops:
  0.6 56.1 %collective-permute-start = (bf16[1024,4096]{1,0:T(8,128)(2,1)}, bf16[1024,4096]{1,0:T(8,128)(2,1)}, u32[]{:S(2)}, u32[]{:S(2)}) collective-permute-start(bf16[1024,4096]{1,0:T(8,128)(2,1)} %refs_0_.1), channel_id=1, source_target_pairs={{0,4},{4,0},{8,12},{12,8},{16,20},{20,16},{24,28},{28,24},{32,36},... | collective-permute-start | bytes 25165832 | tf_op jit(solution)/shard_map/ppermute | solution.py:35
  5.0 7.6 %collective-permute-start.12 = (bf16[16,3200]{1,0:T(8,128)(2,1)S(1)}, bf16[16,3200]{1,0:T(8,128)(2,1)S(1)}, u32[]{:S(2)}, u32[]{:S(2)}) collective-permute-start(bf16[16,3200]{1,0:T(8,128)(2,1)S(1)} %get-tuple-element.14.refs_11_), channel_id=1, source_target_pairs={{0,8},{4,12},{8,16},{12,20},{16,24},{20,28},{24,32},{28,36},{32,40... | collective-permute-start | bytes 307208 | tf_op jit(solution)/shard_map/ppermute | solution.py:35
  5.1 10.0 %collective-permute-start.13 = (bf16[16,3200]{1,0:T(8,128)(2,1)S(1)}, bf16[16,3200]{1,0:T(8,128)(2,1)S(1)}, u32[]{:S(2)}, u32[]{:S(2)}) collective-permute-start(bf16[16,3200]{1,0:T(8,128)(2,1)S(1)} %get-tuple-element.14.refs_11_), channel_id=1, source_target_pairs={{0,56},{4,60},{8,0},{12,4},{16,8},{20,12},{24,16},{28,20},{32,24},... | collective-permute-start | bytes 307208 | tf_op jit(solution)/shard_map/ppermute | solution.py:35
  9.1 7.2 %collective-permute-start.14 = (bf16[16,3200]{1,0:T(8,128)(2,1)S(1)}, bf16[16,3200]{1,0:T(8,128)(2,1)S(1)}, u32[]{:S(2)}, u32[]{:S(2)}) collective-permute-start(bf16[16,3200]{1,0:T(8,128)(2,1)S(1)} %get-tuple-element.14.refs_11_), channel_id=1, source_target_pairs={{0,16},{4,20},{8,24},{12,28},{16,32},{20,36},{24,40},{28,44},{32,4... | collective-permute-start | bytes 307208 | tf_op jit(solution)/shard_map/ppermute | solution.py:35
  9.1 13.2 %collective-permute-start.15 = (bf16[16,3200]{1,0:T(8,128)(2,1)S(1)}, bf16[16,3200]{1,0:T(8,128)(2,1)S(1)}, u32[]{:S(2)}, u32[]{:S(2)}) collective-permute-start(bf16[16,3200]{1,0:T(8,128)(2,1)S(1)} %get-tuple-element.14.refs_11_), channel_id=1, source_target_pairs={{0,48},{4,52},{8,56},{12,60},{16,0},{20,4},{24,8},{28,12},{32,16},... | collective-permute-start | bytes 307208 | tf_op jit(solution)/shard_map/ppermute | solution.py:35
  12.6 6.4 %collective-permute-start.3 = (bf16[16,4224]{1,0:T(8,128)(2,1)S(1)}, bf16[16,4224]{1,0:T(8,128)(2,1)S(1)}, u32[]{:S(2)}, u32[]{:S(2)}) collective-permute-start(bf16[16,4224]{1,0:T(8,128)(2,1)S(1)} %get-tuple-element.12), channel_id=1, source_target_pairs={{0,192},{4,196},{8,200},{12,204},{16,208},{20,212},{24,216},{28,22... | collective-permute-start | bytes 405512 | tf_op jit(solution)/shard_map/ppermute | solution.py:35
  15.1 6.6 %collective-permute-start.2 = (bf16[16,4224]{1,0:T(8,128)(2,1)S(1)}, bf16[16,4224]{1,0:T(8,128)(2,1)S(1)}, u32[]{:S(2)}, u32[]{:S(2)}) collective-permute-start(bf16[16,4224]{1,0:T(8,128)(2,1)S(1)} %get-tuple-element.12), channel_id=1, source_target_pairs={{0,64},{4,68},{8,72},{12,76},{16,80},{20,84},{24,88},{28,92},{32,9... | collective-permute-start | bytes 405512 | tf_op jit(solution)/shard_map/ppermute | solution.py:35
  16.3 5.5 %collective-permute-start.4 = (bf16[16,1024]{1,0:T(8,128)(2,1)S(1)}, bf16[16,1024]{1,0:T(8,128)(2,1)S(1)}, u32[]{:S(2)}, u32[]{:S(2)}) collective-permute-start(bf16[16,1024]{1,0:T(8,128)(2,1)S(1)} %get-tuple-element.13), channel_id=1, source_target_pairs={{0,128},{4,132},{8,136},{12,140},{16,144},{20,148},{24,152},{28,15... | collective-permute-start | bytes 98312 | tf_op jit(solution)/shard_map/ppermute | solution.py:35
  19.0 12.0 %collective-permute-start.1 = (f32[8,128]{1,0:T(8,128)S(1)}, f32[8,128]{1,0:T(8,128)S(1)}, u32[]{:S(2)}, u32[]{:S(2)}) collective-permute-start(f32[8,128]{1,0:T(8,128)S(1)} %get-tuple-element.11.refs_2_), channel_id=1, source_target_pairs={{0,4},{4,0},{8,12},{12,8},{16,20},{20,16},{24,28},{28,24},{32,36},... | collective-permute-start | bytes 12296 | tf_op jit(solution)/shard_map/ppermute | solution.py:35
  21.7 4.8 %collective-permute-start.17 = (bf16[16,3200]{1,0:T(8,128)(2,1)S(1)}, bf16[16,3200]{1,0:T(8,128)(2,1)S(1)}, u32[]{:S(2)}, u32[]{:S(2)}) collective-permute-start(bf16[16,3200]{1,0:T(8,128)(2,1)S(1)} %collective-permute-done.14), channel_id=1, source_target_pairs={{0,8},{4,12},{8,16},{12,20},{16,24},{20,28},{24,32},{28,36},{32,40... | collective-permute-start | bytes 307208 | tf_op jit(solution)/shard_map/ppermute | solution.py:35
  21.8 8.5 %collective-permute-start.19 = (bf16[16,3200]{1,0:T(8,128)(2,1)S(1)}, bf16[16,3200]{1,0:T(8,128)(2,1)S(1)}, u32[]{:S(2)}, u32[]{:S(2)}) collective-permute-start(bf16[16,3200]{1,0:T(8,128)(2,1)S(1)} %collective-permute-done.14), channel_id=1, source_target_pairs={{0,16},{4,20},{8,24},{12,28},{16,32},{20,36},{24,40},{28,44},{32,4... | collective-permute-start | bytes 307208 | tf_op jit(solution)/shard_map/ppermute | solution.py:35
  22.2 6.2 %collective-permute-start.18 = (bf16[16,3200]{1,0:T(8,128)(2,1)S(1)}, bf16[16,3200]{1,0:T(8,128)(2,1)S(1)}, u32[]{:S(2)}, u32[]{:S(2)}) collective-permute-start(bf16[16,3200]{1,0:T(8,128)(2,1)S(1)} %collective-permute-done.15), channel_id=1, source_target_pairs={{0,56},{4,60},{8,0},{12,4},{16,8},{20,12},{24,16},{28,20},{32,24},... | collective-permute-start | bytes 307208 | tf_op jit(solution)/shard_map/ppermute | solution.py:35
  26.5 7.0 %collective-permute-start.7 = (bf16[64,1024]{1,0:T(8,128)(2,1)S(1)}, bf16[64,1024]{1,0:T(8,128)(2,1)S(1)}, u32[]{:S(2)}, u32[]{:S(2)}) collective-permute-start(bf16[64,1024]{1,0:T(8,128)(2,1)S(1)} %pad_maximum_fusion.1.refs_4_.refs_3_), channel_id=1, source_target_pairs={{0,16},{4,20},{8,24},{12,28},{16,32},{20,36},{24,40},{28,44},{32,4... | collective-permute-start | bytes 393224 | tf_op jit(solution)/shard_map/ppermute | solution.py:35
  28.4 9.8 %collective-permute-start.8 = (bf16[64,1024]{1,0:T(8,128)(2,1)S(1)}, bf16[64,1024]{1,0:T(8,128)(2,1)S(1)}, u32[]{:S(2)}, u32[]{:S(2)}) collective-permute-start(bf16[64,1024]{1,0:T(8,128)(2,1)S(1)} %pad_maximum_fusion.1.refs_4_.refs_3_), channel_id=1, source_target_pairs={{0,48},{4,52},{8,56},{12,60},{16,0},{20,4},{24,8},{28,12},{32,16},... | collective-permute-start | bytes 393224 | tf_op jit(solution)/shard_map/ppermute | solution.py:35
  30.2 8.9 %collective-permute-start.5 = (bf16[64,1024]{1,0:T(8,128)(2,1)S(1)}, bf16[64,1024]{1,0:T(8,128)(2,1)S(1)}, u32[]{:S(2)}, u32[]{:S(2)}) collective-permute-start(bf16[64,1024]{1,0:T(8,128)(2,1)S(1)} %pad_maximum_fusion.1.refs_4_.refs_3_), channel_id=1, source_target_pairs={{0,8},{4,12},{8,16},{12,20},{16,24},{20,28},{24,32},{28,36},{32,40... | collective-permute-start | bytes 393224 | tf_op jit(solution)/shard_map/ppermute | solution.py:35
  31.1 8.4 %collective-permute-start.6 = (bf16[64,1024]{1,0:T(8,128)(2,1)S(1)}, bf16[64,1024]{1,0:T(8,128)(2,1)S(1)}, u32[]{:S(2)}, u32[]{:S(2)}) collective-permute-start(bf16[64,1024]{1,0:T(8,128)(2,1)S(1)} %pad_maximum_fusion.1.refs_4_.refs_3_), channel_id=1, source_target_pairs={{0,56},{4,60},{8,0},{12,4},{16,8},{20,12},{24,16},{28,20},{32,24},... | collective-permute-start | bytes 393224 | tf_op jit(solution)/shard_map/ppermute | solution.py:35
  33.5 13.7 %collective-permute-start.22 = (bf16[48,3200]{1,0:T(8,128)(2,1)S(1)}, bf16[48,3200]{1,0:T(8,128)(2,1)S(1)}, u32[]{:S(2)}, u32[]{:S(2)}) collective-permute-start(bf16[48,3200]{1,0:T(8,128)(2,1)S(1)} %constant_dynamic-update-slice_fusion.4.refs_13_), channel_id=1, source_target_pairs={{0,192},{4,196},{8,200},{12,204},{16,208},{20,212},{24,216},{28,22... | collective-permute-start | bytes 921608 | tf_op jit(solution)/shard_map/ppermute | solution.py:35
  38.2 7.6 %collective-permute-start.11 = (bf16[64,1024]{1,0:T(8,128)(2,1)S(1)}, bf16[64,1024]{1,0:T(8,128)(2,1)S(1)}, u32[]{:S(2)}, u32[]{:S(2)}) collective-permute-start(bf16[64,1024]{1,0:T(8,128)(2,1)S(1)} %collective-permute-done.7.refs_7_.refs_6_), channel_id=1, source_target_pairs={{0,16},{4,20},{8,24},{12,28},{16,32},{20,36},{24,40},{28,44},{32,4... | collective-permute-start | bytes 393224 | tf_op jit(solution)/shard_map/ppermute | solution.py:35
  39.2 7.0 %collective-permute-start.9 = (bf16[64,1024]{1,0:T(8,128)(2,1)S(1)}, bf16[64,1024]{1,0:T(8,128)(2,1)S(1)}, u32[]{:S(2)}, u32[]{:S(2)}) collective-permute-start(bf16[64,1024]{1,0:T(8,128)(2,1)S(1)} %collective-permute-done.7.refs_7_.refs_6_), channel_id=1, source_target_pairs={{0,8},{4,12},{8,16},{12,20},{16,24},{20,28},{24,32},{28,36},{32,40... | collective-permute-start | bytes 393224 | tf_op jit(solution)/shard_map/ppermute | solution.py:35
  39.5 14.5 %collective-permute-start.16 = (bf16[64,3200]{1,0:T(8,128)(2,1)S(1)}, bf16[64,3200]{1,0:T(8,128)(2,1)S(1)}, u32[]{:S(2)}, u32[]{:S(2)}) collective-permute-start(bf16[64,3200]{1,0:T(8,128)(2,1)S(1)} %constant_dynamic-update-slice_fusion.refs_12_), channel_id=1, source_target_pairs={{0,64},{4,68},{8,72},{12,76},{16,80},{20,84},{24,88},{28,92},{32,9... | collective-permute-start | bytes 1228808 | tf_op jit(solution)/shard_map/ppermute | solution.py:35
  45.8 8.2 %collective-permute-start.21 = (bf16[64,3200]{1,0:T(8,128)(2,1)S(1)}, bf16[64,3200]{1,0:T(8,128)(2,1)S(1)}, u32[]{:S(2)}, u32[]{:S(2)}) collective-permute-start(bf16[64,3200]{1,0:T(8,128)(2,1)S(1)} %constant_dynamic-update-slice_fusion.refs_12_), channel_id=1, source_target_pairs={{0,192},{4,196},{8,200},{12,204},{16,208},{20,212},{24,216},{28,22... | collective-permute-start | bytes 1228808 | tf_op jit(solution)/shard_map/ppermute | solution.py:35
  46.2 10.5 %collective-permute-start.20 = (bf16[48,3200]{1,0:T(8,128)(2,1)S(1)}, bf16[48,3200]{1,0:T(8,128)(2,1)S(1)}, u32[]{:S(2)}, u32[]{:S(2)}) collective-permute-start(bf16[48,3200]{1,0:T(8,128)(2,1)S(1)} %constant_dynamic-update-slice_fusion.4.refs_13_), channel_id=1, source_target_pairs={{0,64},{4,68},{8,72},{12,76},{16,80},{20,84},{24,88},{28,92},{32,9... | collective-permute-start | bytes 921608 | tf_op jit(solution)/shard_map/ppermute | solution.py:35
  47.2 4.1 %collective-permute-start.10 = (bf16[64,1024]{1,0:T(8,128)(2,1)S(1)}, bf16[64,1024]{1,0:T(8,128)(2,1)S(1)}, u32[]{:S(2)}, u32[]{:S(2)}) collective-permute-start(bf16[64,1024]{1,0:T(8,128)(2,1)S(1)} %collective-permute-done.8.refs_8_.refs_7_), channel_id=1, source_target_pairs={{0,56},{4,60},{8,0},{12,4},{16,8},{20,12},{24,16},{28,20},{32,24},... | collective-permute-start | bytes 393224 | tf_op jit(solution)/shard_map/ppermute | solution.py:35
  51.4 16.0 %collective-permute-start.24 = (bf16[64,3200]{1,0:T(8,128)(2,1)S(1)}, bf16[64,3200]{1,0:T(8,128)(2,1)S(1)}, u32[]{:S(2)}, u32[]{:S(2)}) collective-permute-start(bf16[64,3200]{1,0:T(8,128)(2,1)S(1)} %pad_maximum_fusion), channel_id=1, source_target_pairs={{0,192},{4,196},{8,200},{12,204},{16,208},{20,212},{24,216},{28,22... | collective-permute-start | bytes 1228808 | tf_op jit(solution)/shard_map/ppermute | solution.py:35
  54.0 13.3 %collective-permute-start.23 = (bf16[64,3200]{1,0:T(8,128)(2,1)S(1)}, bf16[64,3200]{1,0:T(8,128)(2,1)S(1)}, u32[]{:S(2)}, u32[]{:S(2)}) collective-permute-start(bf16[64,3200]{1,0:T(8,128)(2,1)S(1)} %collective-permute-done.16.refs_13_), channel_id=1, source_target_pairs={{0,64},{4,68},{8,72},{12,76},{16,80},{20,84},{24,88},{28,92},{32,9... | collective-permute-start | bytes 1228808 | tf_op jit(solution)/shard_map/ppermute | solution.py:35
  74.0 16.9 %all-to-all-start = ((f32[32,8,128]{2,1,0:T(8,128)}), f32[32,8,128]{2,1,0:T(8,128)S(1)}, u32[]{:S(2)}, u32[]{:S(2)}) async-start(f32[32,8,128]{2,1,0:T(8,128)} %shard_map.61), calls=%async_computation | async-start | bytes 262144 | tf_op jit(solution)/shard_map/all_to_all | solution.py:276
  91.6 14.2 %all-to-all-start.1 = ((f32[8,1,128]{2,1,0:T(1,128)}), f32[8,1,128]{2,1,0:T(1,128)S(1)}, u32[]{:S(2)}, u32[]{:S(2)}) async-start(f32[8,1,128]{2,1,0:T(1,128)} %get-tuple-element.19), calls=%async_computation.1 | async-start | bytes 8192 | tf_op jit(solution)/shard_map/all_to_all | solution.py:286
where the time goes:
time: 108 us
  starting transfers between devices  57.9 us (54%)
  waiting for transfers between devices  27.3 us (25%)
  Pallas kernels  19.1 us (18%)
  between operations  2.61 us (2%)
    ppermute x25, starting transfers between devices, shift(): return lax.ppermute(array, 'vocab', pairs)  40.5 us
    pallas_call x4, Pallas kernels, call(): pl.pallas_call(kernel, out_shape=out_shape, in_specs=specs or [VMEM] * le...  19.1 us
    ppermute x25, waiting for transfers between devices, shift(): return lax.ppermute(array, 'vocab', pairs)  14.2 us
    all_to_all x1, starting transfers between devices, head_loss(): lax.all_to_all(summed, ('vocab', 'seq'), 0, 0, tiled=True, axis_index_gro...  9.61 us
    all_to_all x1, waiting for transfers between devices, head_loss(): lax.all_to_all(pieces, 'vocab', 0, 0, tiled=True, axis_index_groups=same_...  9.1 us
    all_to_all x1, starting transfers between devices, head_loss(): lax.all_to_all(pieces, 'vocab', 0, 0, tiled=True, axis_index_groups=same_...  7.75 us
    all_to_all x1, waiting for transfers between devices, head_loss(): lax.all_to_all(summed, ('vocab', 'seq'), 0, 0, tiled=True, axis_index_gro...  4.01 us
  transfers between devices with their start and end apart: 27, of which 10 were waited for; matrix products, arithmetic and copies ran while one was open for 1% of the time, Pallas kernels for 11%

commit v1 on v0

--- a/solution.py
+++ b/solution.py
@@ -11,12 +11,12 @@
 epsilon = 1e-06
 NX, NZ, NC, NY = 4, 8, 2, 4
 D = 4096
-CA = 1024
+CA = 768
 CB = D - CA
 CT = 128
 ROWS = 16
 HALF = NZ * ROWS
-BLOCK = 512
+BLOCK = 256
 f32, bf16 = jnp.float32, jnp.bfloat16
 VMEM = pl.BlockSpec(memory_space=pltpu.VMEM)
 
@@ -84,6 +84,7 @@
 
 def head_kernel(a_spots, b_spots, last, counts, *refs):
     n_a, n_b = counts
+    block = 4 * BLOCK if last else BLOCK
     if last:
         tables, gains, first_ref, *rest = refs
     else:
@@ -94,14 +95,14 @@
     else:
         out_ref, tables, gains, tokens, coded, logits, scales, arrived = rest
     rows = tables.shape[0] // 2
-    blocks = 2 * rows // BLOCK
+    blocks = 2 * rows // block
 
     if not last:
         for k in range(blocks):
-            source = (own_ref, swapped_ref)[k * BLOCK // rows]
-            at = pl.ds(k * BLOCK % rows, BLOCK)
+            source = (own_ref, swapped_ref)[k * block // rows]
+            at = pl.ds(k * block % rows, block)
             pltpu.make_async_copy(
-                source.at[at], tables.at[pl.ds(k * BLOCK, BLOCK)], arrived.at[k]
+                source.at[at], tables.at[pl.ds(k * block, block)], arrived.at[k]
             ).start()
         scales[: rows // 128, :] = own_scale[...]
         scales[rows // 128 :, :] = swapped_scale[...]
@@ -123,17 +124,17 @@
 
     def step(k, carry):
         peak, picked = carry
-        part = pl.ds(pl.multiple_of(k * BLOCK, BLOCK), BLOCK)
+        part = pl.ds(pl.multiple_of(k * block, block), block)
         if not last:
-            pltpu.make_async_copy(own_ref.at[pl.ds(0, BLOCK)], tables.at[part], arrived.at[k]).wait()
-            for j in range(BLOCK // 128):
-                some = pl.ds(pl.multiple_of(k * BLOCK + j * 128, 128), 128)
+            pltpu.make_async_copy(own_ref.at[pl.ds(0, block)], tables.at[part], arrived.at[k]).wait()
+            for j in range(block // 128):
+                some = pl.ds(pl.multiple_of(k * block + j * 128, 128), 128)
                 total = jnp.zeros((128, 128), f32)
                 for i in range(D // 128):
                     piece = tables[some, i * 128 : (i + 1) * 128].astype(f32)
                     total += piece * piece
                 norm = lax.rsqrt(jnp.sum(total, axis=1, keepdims=True) + epsilon)
-                scale = scales[pl.ds(k * (BLOCK // 128) + j, 1), :]
+                scale = scales[pl.ds(k * (block // 128) + j, 1), :]
                 gains[some, :] = norm * jnp.broadcast_to(scale, (128, 128)).T
         value = lax.dot_general(
             tables[part, :], tokens[...], (((1,), (1,)), ((), ())), preferred_element_type=f32
@@ -141,11 +142,11 @@
         factor = gains[part, :]
         value = value * jnp.concatenate([factor, factor], axis=1)
         logits[part, :] = value
-        base = jnp.where(k * BLOCK < rows, own_base, swapped_base) + k * BLOCK
-        row = lax.broadcasted_iota(jnp.int32, (BLOCK, 256), 0)
+        base = jnp.where(k * block < rows, own_base, swapped_base) + k * block
+        row = lax.broadcasted_iota(jnp.int32, (block, 256), 0)
         chosen = jnp.where(row == target - base, value, 0.0)
-        peak = jnp.maximum(peak, jnp.max(value.reshape(BLOCK // 8, 8, 256), axis=0))
-        picked = picked + jnp.sum(chosen.reshape(BLOCK // 8, 8, 256), axis=0)
+        peak = jnp.maximum(peak, jnp.max(value.reshape(block // 8, 8, 256), axis=0))
+        picked = picked + jnp.sum(chosen.reshape(block // 8, 8, 256), axis=0)
         return peak, picked
 
     peak, picked = lax.fori_loop(

time: 108 us -> 112 us (1.037)
  waiting for transfers between devices: 27.3 us -> 33.4 us
  starting transfers between devices: 57.9 us -> 55.2 us
    ppermute x25, starting transfers between devices: 40.5 us -> 34.4 us  [shift(): return lax.ppermute(array, 'vocab', pairs)]
    ppermute x25, waiting for transfers between devices: 14.2 us -> 20.3 us  [shift(): return lax.ppermute(array, 'vocab', pairs)]
    all_to_all x1, starting transfers between devices: 9.61 us -> 14.8 us  [head_loss(): lax.all_to_all(summed, ('vocab', 'seq'), 0, 0, tiled=True, axis_index_gro...]
    all_to_all x1, starting transfers between devices: 7.75 us -> 5.93 us  [head_loss(): lax.all_to_all(pieces, 'vocab', 0, 0, tiled=True, axis_index_groups=same_...]
where the time goes in v1:
time: 112 us
  starting transfers between devices  55.2 us (49%)
  waiting for transfers between devices  33.4 us (30%)
  Pallas kernels  19.3 us (17%)
  between operations  2.61 us (2%)
    ppermute x25, starting transfers between devices, shift(): return lax.ppermute(array, 'vocab', pairs)  34.4 us
    ppermute x25, waiting for transfers between devices, shift(): return lax.ppermute(array, 'vocab', pairs)  20.3 us
    pallas_call x4, Pallas kernels, call(): pl.pallas_call(kernel, out_shape=out_shape, in_specs=specs or [VMEM] * le...  19.3 us
    all_to_all x1, starting transfers between devices, head_loss(): lax.all_to_all(summed, ('vocab', 'seq'), 0, 0, tiled=True, axis_index_gro...  14.8 us
    all_to_all x1, waiting for transfers between devices, head_loss(): lax.all_to_all(pieces, 'vocab', 0, 0, tiled=True, axis_index_groups=same_...  9.1 us
    all_to_all x1, starting transfers between devices, head_loss(): lax.all_to_all(pieces, 'vocab', 0, 0, tiled=True, axis_index_groups=same_...  5.93 us
    all_to_all x1, waiting for transfers between devices, head_loss(): lax.all_to_all(summed, ('vocab', 'seq'), 0, 0, tiled=True, axis_index_gro...  4.01 us
  transfers between devices with their start and end apart: 27, of which 10 were waited for; matrix products, arithmetic and copies ran while one was open for 1% of the time, Pallas kernels for 11%

profile of v1, /device:TPU:1, one launch (start us, length us, event | category | flops | bytes accessed | tf_op | source)
XLA Modules:
  0.0 111.8 jit_solution(836947722357840508)
XLA Ops:
  0.6 3.3 %collective-permute-start = (bf16[1024,4096]{1,0:T(8,128)(2,1)}, bf16[1024,4096]{1,0:T(8,128)(2,1)}, u32[]{:S(2)}, u32[]{:S(2)}) collective-permute-start(bf16[1024,4096]{1,0:T(8,128)(2,1)} %refs_0_.1), channel_id=1, source_target_pairs={{0,4},{4,0},{8,12},{12,8},{16,20},{20,16},{24,28},{28,24},{32,36},... | collective-permute-start | bytes 25165832 | tf_op jit(solution)/shard_map/ppermute | solution.py:35
  3.9 1.1 shard_map.59
  5.1 3.9 %collective-permute-start.13 = (bf16[16,3456]{1,0:T(8,128)(2,1)S(1)}, bf16[16,3456]{1,0:T(8,128)(2,1)S(1)}, u32[]{:S(2)}, u32[]{:S(2)}) collective-permute-start(bf16[16,3456]{1,0:T(8,128)(2,1)S(1)} %get-tuple-element.14.refs_11_), channel_id=1, source_target_pairs={{0,56},{4,60},{8,0},{12,4},{16,8},{20,12},{24,16},{28,20},{32,24},... | collective-permute-start | bytes 331784 | tf_op jit(solution)/shard_map/ppermute | solution.py:35
  9.1 3.6 %collective-permute-start.15 = (bf16[16,3456]{1,0:T(8,128)(2,1)S(1)}, bf16[16,3456]{1,0:T(8,128)(2,1)S(1)}, u32[]{:S(2)}, u32[]{:S(2)}) collective-permute-start(bf16[16,3456]{1,0:T(8,128)(2,1)S(1)} %get-tuple-element.14.refs_11_), channel_id=1, source_target_pairs={{0,48},{4,52},{8,56},{12,60},{16,0},{20,4},{24,8},{28,12},{32,16},... | collective-permute-start | bytes 331784 | tf_op jit(solution)/shard_map/ppermute | solution.py:35
  12.6 2.5 %collective-permute-start.3 = (bf16[16,4224]{1,0:T(8,128)(2,1)S(1)}, bf16[16,4224]{1,0:T(8,128)(2,1)S(1)}, u32[]{:S(2)}, u32[]{:S(2)}) collective-permute-start(bf16[16,4224]{1,0:T(8,128)(2,1)S(1)} %get-tuple-element.12), channel_id=1, source_target_pairs={{0,192},{4,196},{8,200},{12,204},{16,208},{20,212},{24,216},{28,22... | collective-permute-start | bytes 405512 | tf_op jit(solution)/shard_map/ppermute | solution.py:35
  15.2 1.2 %collective-permute-done.14 = bf16[16,3456]{1,0:T(8,128)(2,1)S(1)} collective-permute-done((bf16[16,3456]{1,0:T(8,128)(2,1)S(1)}, bf16[16,3456]{1,0:T(8,128)(2,1)S(1)}, u32[]{:S(2)}, u32[]{:S(2)}) %collective-permute-start.14) | collective-permute-done | bytes 110624 | tf_op jit(solution)/shard_map/ppermute | solution.py:35
  16.4 2.7 %collective-permute-start.4 = (bf16[16,768]{1,0:T(8,128)(2,1)S(1)}, bf16[16,768]{1,0:T(8,128)(2,1)S(1)}, u32[]{:S(2)}, u32[]{:S(2)}) collective-permute-start(bf16[16,768]{1,0:T(8,128)(2,1)S(1)} %get-tuple-element.13), channel_id=1, source_target_pairs={{0,128},{4,132},{8,136},{12,140},{16,144},{20,148},{24,152},{28,15... | collective-permute-start | bytes 73736 | tf_op jit(solution)/shard_map/ppermute | solution.py:35
  19.2 2.9 %collective-permute-start.1 = (f32[8,128]{1,0:T(8,128)S(1)}, f32[8,128]{1,0:T(8,128)S(1)}, u32[]{:S(2)}, u32[]{:S(2)}) collective-permute-start(f32[8,128]{1,0:T(8,128)S(1)} %get-tuple-element.11.refs_2_), channel_id=1, source_target_pairs={{0,4},{4,0},{8,12},{12,8},{16,20},{20,16},{24,28},{28,24},{32,36},... | collective-permute-start | bytes 12296 | tf_op jit(solution)/shard_map/ppermute | solution.py:35
  22.5 2.4 %collective-permute-start.18 = (bf16[16,3456]{1,0:T(8,128)(2,1)S(1)}, bf16[16,3456]{1,0:T(8,128)(2,1)S(1)}, u32[]{:S(2)}, u32[]{:S(2)}) collective-permute-start(bf16[16,3456]{1,0:T(8,128)(2,1)S(1)} %collective-permute-done.15), channel_id=1, source_target_pairs={{0,56},{4,60},{8,0},{12,4},{16,8},{20,12},{24,16},{28,20},{32,24},... | collective-permute-start | bytes 331784 | tf_op jit(solution)/shard_map/ppermute | solution.py:35
  24.9 2.7 %collective-permute-done.17 = bf16[16,3456]{1,0:T(8,128)(2,1)S(1)} collective-permute-done((bf16[16,3456]{1,0:T(8,128)(2,1)S(1)}, bf16[16,3456]{1,0:T(8,128)(2,1)S(1)}, u32[]{:S(2)}, u32[]{:S(2)}) %collective-permute-start.17) | collective-permute-done | bytes 110624 | tf_op jit(solution)/shard_map/ppermute | solution.py:35
  27.8 1.1 %collective-permute-done.18 = bf16[16,3456]{1,0:T(8,128)(2,1)S(1)} collective-permute-done((bf16[16,3456]{1,0:T(8,128)(2,1)S(1)}, bf16[16,3456]{1,0:T(8,128)(2,1)S(1)}, u32[]{:S(2)}, u32[]{:S(2)}) %collective-permute-start.18) | collective-permute-done | bytes 110624 | tf_op jit(solution)/shard_map/ppermute | solution.py:35
  28.9 2.3 %collective-permute-start.8 = (bf16[64,768]{1,0:T(8,128)(2,1)S(1)}, bf16[64,768]{1,0:T(8,128)(2,1)S(1)}, u32[]{:S(2)}, u32[]{:S(2)}) collective-permute-start(bf16[64,768]{1,0:T(8,128)(2,1)S(1)} %pad_maximum_fusion.1.refs_4_.refs_3_), channel_id=1, source_target_pairs={{0,48},{4,52},{8,56},{12,60},{16,0},{20,4},{24,8},{28,12},{32,16},... | collective-permute-start | bytes 294920 | tf_op jit(solution)/shard_map/ppermute | solution.py:35
  31.2 2.0 %collective-permute-start.5 = (bf16[64,768]{1,0:T(8,128)(2,1)S(1)}, bf16[64,768]{1,0:T(8,128)(2,1)S(1)}, u32[]{:S(2)}, u32[]{:S(2)}) collective-permute-start(bf16[64,768]{1,0:T(8,128)(2,1)S(1)} %pad_maximum_fusion.1.refs_4_.refs_3_), channel_id=1, source_target_pairs={{0,8},{4,12},{8,16},{12,20},{16,24},{20,28},{24,32},{28,36},{32,40... | collective-permute-start | bytes 294920 | tf_op jit(solution)/shard_map/ppermute | solution.py:35
  33.2 1.0 collective-permute-start.6
  34.3 2.4 %collective-permute-done.7.refs_7_.refs_6_ = bf16[64,768]{1,0:T(8,128)(2,1)S(1)} collective-permute-done((bf16[64,768]{1,0:T(8,128)(2,1)S(1)}, bf16[64,768]{1,0:T(8,128)(2,1)S(1)}, u32[]{:S(2)}, u32[]{:S(2)}) %collective-permute-start.7) | collective-permute-done | bytes 98336 | tf_op jit(solution)/shard_map/ppermute | solution.py:35
  36.7 2.0 %collective-permute-start.22 = (bf16[48,3456]{1,0:T(8,128)(2,1)S(1)}, bf16[48,3456]{1,0:T(8,128)(2,1)S(1)}, u32[]{:S(2)}, u32[]{:S(2)}) collective-permute-start(bf16[48,3456]{1,0:T(8,128)(2,1)S(1)} %constant_dynamic-update-slice_fusion.4.refs_13_), channel_id=1, source_target_pairs={{0,192},{4,196},{8,200},{12,204},{16,208},{20,212},{24,216},{28,22... | collective-permute-start | bytes 995336 | tf_op jit(solution)/shard_map/ppermute | solution.py:35
  38.7 0.7 collective-permute-start.9
  40.0 5.7 %collective-permute-done.11.refs_11_.refs_10_ = bf16[64,768]{1,0:T(8,128)(2,1)S(1)} collective-permute-done((bf16[64,768]{1,0:T(8,128)(2,1)S(1)}, bf16[64,768]{1,0:T(8,128)(2,1)S(1)}, u32[]{:S(2)}, u32[]{:S(2)}) %collective-permute-start.11) | collective-permute-done | bytes 98336 | tf_op jit(solution)/shard_map/ppermute | solution.py:35
  45.7 1.5 %collective-permute-start.20 = (bf16[48,3456]{1,0:T(8,128)(2,1)S(1)}, bf16[48,3456]{1,0:T(8,128)(2,1)S(1)}, u32[]{:S(2)}, u32[]{:S(2)}) collective-permute-start(bf16[48,3456]{1,0:T(8,128)(2,1)S(1)} %constant_dynamic-update-slice_fusion.4.refs_13_), channel_id=1, source_target_pairs={{0,64},{4,68},{8,72},{12,76},{16,80},{20,84},{24,88},{28,92},{32,9... | collective-permute-start | bytes 995336 | tf_op jit(solution)/shard_map/ppermute | solution.py:35
  47.1 0.9 collective-permute-start.10
  48.1 2.8 %collective-permute-done.10.refs_10_.refs_9_ = bf16[64,768]{1,0:T(8,128)(2,1)S(1)} collective-permute-done((bf16[64,768]{1,0:T(8,128)(2,1)S(1)}, bf16[64,768]{1,0:T(8,128)(2,1)S(1)}, u32[]{:S(2)}, u32[]{:S(2)}) %collective-permute-start.10) | collective-permute-done | bytes 98336 | tf_op jit(solution)/shard_map/ppermute | solution.py:35
  50.9 1.5 %collective-permute-start.24 = (bf16[64,3456]{1,0:T(8,128)(2,1)S(1)}, bf16[64,3456]{1,0:T(8,128)(2,1)S(1)}, u32[]{:S(2)}, u32[]{:S(2)}) collective-permute-start(bf16[64,3456]{1,0:T(8,128)(2,1)S(1)} %pad_maximum_fusion), channel_id=1, source_target_pairs={{0,192},{4,196},{8,200},{12,204},{16,208},{20,212},{24,216},{28,22... | collective-permute-start | bytes 1327112 | tf_op jit(solution)/shard_map/ppermute | solution.py:35
  52.4 2.2 %collective-permute-done.21.refs_16_ = bf16[64,3456]{1,0:T(8,128)(2,1)S(1)} collective-permute-done((bf16[64,3456]{1,0:T(8,128)(2,1)S(1)}, bf16[64,3456]{1,0:T(8,128)(2,1)S(1)}, u32[]{:S(2)}, u32[]{:S(2)}) %collective-permute-start.21) | collective-permute-done | bytes 442400 | tf_op jit(solution)/shard_map/ppermute | solution.py:35
  54.6 2.1 %collective-permute-done.20.refs_14_ = bf16[48,3456]{1,0:T(8,128)(2,1)S(1)} collective-permute-done((bf16[48,3456]{1,0:T(8,128)(2,1)S(1)}, bf16[48,3456]{1,0:T(8,128)(2,1)S(1)}, u32[]{:S(2)}, u32[]{:S(2)}) %collective-permute-start.20) | collective-permute-done | bytes 331808 | tf_op jit(solution)/shard_map/ppermute | solution.py:35
  56.7 11.2 %shard_map.60 = (f32[8,128]{1,0:T(8,128)S(1)}, bf16[2048,4096]{1,0:T(8,128)(2,1)S(1)}, f32[2048,128]{1,0:T(8,128)S(1)}) custom-call(bf16[1024,4096]{1,0:T(8,128)(2,1)} %refs_0_.1, bf16[1024,4096]{1,0:T(8,128)(2,1)} %collective-permute-done.refs_1_, f32[8,128]{1,0:T(8,128)S(1)} %get-tuple-element.11.refs_2_, f32[8,128]{1,0:T(8,128)S(1)} %collective-permute-done.1.refs_3_, ...), custom_call_target="tpu_custom_call" | custom-call | flops 4294967296 | bytes 67108864 | tf_op jit(solution)/shard_map/pallas_call | solution.py:39
  68.0 6.2 %shard_map.61 = f32[32,8,128]{2,1,0:T(8,128)} custom-call(bf16[2048,4096]{1,0:T(8,128)(2,1)S(1)} %get-tuple-element.15.refs_0_, f32[2048,128]{1,0:T(8,128)S(1)} %get-tuple-element.16.refs_1_, f32[8,128]{1,0:T(8,128)S(1)} %get-tuple-element.17.refs_2_, bf16[64,768]{1,0:T(8,128)(2,1)S(1)} %pad_maximum_fusion.1.refs_4_.refs_3_, ...), custom_call_target="tpu_custom_call" | custom-call | flops 4294967296 | bytes 67108864 | tf_op jit(solution)/shard_map/pallas_call | solution.py:39
  74.2 5.9 %all-to-all-start = ((f32[32,8,128]{2,1,0:T(8,128)}), f32[32,8,128]{2,1,0:T(8,128)S(1)}, u32[]{:S(2)}, u32[]{:S(2)}) async-start(f32[32,8,128]{2,1,0:T(8,128)} %shard_map.61), calls=%async_computation | async-start | bytes 262144 | tf_op jit(solution)/shard_map/all_to_all | solution.py:277
  80.1 9.1 %all-to-all-done.pieces_ref = f32[32,8,128]{2,1,0:T(8,128)S(1)} async-done(((f32[32,8,128]{2,1,0:T(8,128)}), f32[32,8,128]{2,1,0:T(8,128)S(1)}, u32[]{:S(2)}, u32[]{:S(2)}) %all-to-all-start) | async-done | bytes 131104 | tf_op jit(solution)/shard_map/all_to_all | solution.py:277
  89.2 0.7 shard_map.62
  90.0 14.8 %all-to-all-start.1 = ((f32[8,1,128]{2,1,0:T(1,128)}), f32[8,1,128]{2,1,0:T(1,128)S(1)}, u32[]{:S(2)}, u32[]{:S(2)}) async-start(f32[8,1,128]{2,1,0:T(1,128)} %get-tuple-element.19), calls=%async_computation.1 | async-start | bytes 8192 | tf_op jit(solution)/shard_map/all_to_all | solution.py:287
  105.4 4.0 %all-to-all-done.1 = f32[8,1,128]{2,1,0:T(1,128)S(1)} async-done(((f32[8,1,128]{2,1,0:T(1,128)}), f32[8,1,128]{2,1,0:T(1,128)S(1)}, u32[]{:S(2)}, u32[]{:S(2)}) %all-to-all-start.1) | async-done | bytes 4128 | tf_op jit(solution)/shard_map/all_to_all | solution.py:287
  109.4 0.6 slice_reduce_fusion
  (40 shorter events, 2.0 us)
Async XLA Ops:
  0.6 56.1 %collective-permute-start = (bf16[1024,4096]{1,0:T(8,128)(2,1)}, bf16[1024,4096]{1,0:T(8,128)(2,1)}, u32[]{:S(2)}, u32[]{:S(2)}) collective-permute-start(bf16[1024,4096]{1,0:T(8,128)(2,1)} %refs_0_.1), channel_id=1, source_target_pairs={{0,4},{4,0},{8,12},{12,8},{16,20},{20,16},{24,28},{28,24},{32,36},... | collective-permute-start | bytes 25165832 | tf_op jit(solution)/shard_map/ppermute | solution.py:35
  5.0 7.6 %collective-permute-start.12 = (bf16[16,3456]{1,0:T(8,128)(2,1)S(1)}, bf16[16,3456]{1,0:T(8,128)(2,1)S(1)}, u32[]{:S(2)}, u32[]{:S(2)}) collective-permute-start(bf16[16,3456]{1,0:T(8,128)(2,1)S(1)} %get-tuple-element.14.refs_11_), channel_id=1, source_target_pairs={{0,8},{4,12},{8,16},{12,20},{16,24},{20,28},{24,32},{28,36},{32,40... | collective-permute-start | bytes 331784 | tf_op jit(solution)/shard_map/ppermute | solution.py:35
  5.1 10.0 %collective-permute-start.13 = (bf16[16,3456]{1,0:T(8,128)(2,1)S(1)}, bf16[16,3456]{1,0:T(8,128)(2,1)S(1)}, u32[]{:S(2)}, u32[]{:S(2)}) collective-permute-start(bf16[16,3456]{1,0:T(8,128)(2,1)S(1)} %get-tuple-element.14.refs_11_), channel_id=1, source_target_pairs={{0,56},{4,60},{8,0},{12,4},{16,8},{20,12},{24,16},{28,20},{32,24},... | collective-permute-start | bytes 331784 | tf_op jit(solution)/shard_map/ppermute | solution.py:35
  9.1 7.4 %collective-permute-start.14 = (bf16[16,3456]{1,0:T(8,128)(2,1)S(1)}, bf16[16,3456]{1,0:T(8,128)(2,1)S(1)}, u32[]{:S(2)}, u32[]{:S(2)}) collective-permute-start(bf16[16,3456]{1,0:T(8,128)(2,1)S(1)} %get-tuple-element.14.refs_11_), channel_id=1, source_target_pairs={{0,16},{4,20},{8,24},{12,28},{16,32},{20,36},{24,40},{28,44},{32,4... | collective-permute-start | bytes 331784 | tf_op jit(solution)/shard_map/ppermute | solution.py:35
  9.1 13.4 %collective-permute-start.15 = (bf16[16,3456]{1,0:T(8,128)(2,1)S(1)}, bf16[16,3456]{1,0:T(8,128)(2,1)S(1)}, u32[]{:S(2)}, u32[]{:S(2)}) collective-permute-start(bf16[16,3456]{1,0:T(8,128)(2,1)S(1)} %get-tuple-element.14.refs_11_), channel_id=1, source_target_pairs={{0,48},{4,52},{8,56},{12,60},{16,0},{20,4},{24,8},{28,12},{32,16},... | collective-permute-start | bytes 331784 | tf_op jit(solution)/shard_map/ppermute | solution.py:35
  12.6 6.6 %collective-permute-start.3 = (bf16[16,4224]{1,0:T(8,128)(2,1)S(1)}, bf16[16,4224]{1,0:T(8,128)(2,1)S(1)}, u32[]{:S(2)}, u32[]{:S(2)}) collective-permute-start(bf16[16,4224]{1,0:T(8,128)(2,1)S(1)} %get-tuple-element.12), channel_id=1, source_target_pairs={{0,192},{4,196},{8,200},{12,204},{16,208},{20,212},{24,216},{28,22... | collective-permute-start | bytes 405512 | tf_op jit(solution)/shard_map/ppermute | solution.py:35
  15.1 7.0 %collective-permute-start.2 = (bf16[16,4224]{1,0:T(8,128)(2,1)S(1)}, bf16[16,4224]{1,0:T(8,128)(2,1)S(1)}, u32[]{:S(2)}, u32[]{:S(2)}) collective-permute-start(bf16[16,4224]{1,0:T(8,128)(2,1)S(1)} %get-tuple-element.12), channel_id=1, source_target_pairs={{0,64},{4,68},{8,72},{12,76},{16,80},{20,84},{24,88},{28,92},{32,9... | collective-permute-start | bytes 405512 | tf_op jit(solution)/shard_map/ppermute | solution.py:35
  16.4 5.7 %collective-permute-start.4 = (bf16[16,768]{1,0:T(8,128)(2,1)S(1)}, bf16[16,768]{1,0:T(8,128)(2,1)S(1)}, u32[]{:S(2)}, u32[]{:S(2)}) collective-permute-start(bf16[16,768]{1,0:T(8,128)(2,1)S(1)} %get-tuple-element.13), channel_id=1, source_target_pairs={{0,128},{4,132},{8,136},{12,140},{16,144},{20,148},{24,152},{28,15... | collective-permute-start | bytes 73736 | tf_op jit(solution)/shard_map/ppermute | solution.py:35
  19.2 14.0 %collective-permute-start.1 = (f32[8,128]{1,0:T(8,128)S(1)}, f32[8,128]{1,0:T(8,128)S(1)}, u32[]{:S(2)}, u32[]{:S(2)}) collective-permute-start(f32[8,128]{1,0:T(8,128)S(1)} %get-tuple-element.11.refs_2_), channel_id=1, source_target_pairs={{0,4},{4,0},{8,12},{12,8},{16,20},{20,16},{24,28},{28,24},{32,36},... | collective-permute-start | bytes 12296 | tf_op jit(solution)/shard_map/ppermute | solution.py:35
  22.1 5.5 %collective-permute-start.17 = (bf16[16,3456]{1,0:T(8,128)(2,1)S(1)}, bf16[16,3456]{1,0:T(8,128)(2,1)S(1)}, u32[]{:S(2)}, u32[]{:S(2)}) collective-permute-start(bf16[16,3456]{1,0:T(8,128)(2,1)S(1)} %collective-permute-done.14), channel_id=1, source_target_pairs={{0,8},{4,12},{8,16},{12,20},{16,24},{20,28},{24,32},{28,36},{32,40... | collective-permute-start | bytes 331784 | tf_op jit(solution)/shard_map/ppermute | solution.py:35
  22.1 9.1 %collective-permute-start.19 = (bf16[16,3456]{1,0:T(8,128)(2,1)S(1)}, bf16[16,3456]{1,0:T(8,128)(2,1)S(1)}, u32[]{:S(2)}, u32[]{:S(2)}) collective-permute-start(bf16[16,3456]{1,0:T(8,128)(2,1)S(1)} %collective-permute-done.14), channel_id=1, source_target_pairs={{0,16},{4,20},{8,24},{12,28},{16,32},{20,36},{24,40},{28,44},{32,4... | collective-permute-start | bytes 331784 | tf_op jit(solution)/shard_map/ppermute | solution.py:35
  22.5 6.4 %collective-permute-start.18 = (bf16[16,3456]{1,0:T(8,128)(2,1)S(1)}, bf16[16,3456]{1,0:T(8,128)(2,1)S(1)}, u32[]{:S(2)}, u32[]{:S(2)}) collective-permute-start(bf16[16,3456]{1,0:T(8,128)(2,1)S(1)} %collective-permute-done.15), channel_id=1, source_target_pairs={{0,56},{4,60},{8,0},{12,4},{16,8},{20,12},{24,16},{28,20},{32,24},... | collective-permute-start | bytes 331784 | tf_op jit(solution)/shard_map/ppermute | solution.py:35
  27.5 9.1 %collective-permute-start.7 = (bf16[64,768]{1,0:T(8,128)(2,1)S(1)}, bf16[64,768]{1,0:T(8,128)(2,1)S(1)}, u32[]{:S(2)}, u32[]{:S(2)}) collective-permute-start(bf16[64,768]{1,0:T(8,128)(2,1)S(1)} %pad_maximum_fusion.1.refs_4_.refs_3_), channel_id=1, source_target_pairs={{0,16},{4,20},{8,24},{12,28},{16,32},{20,36},{24,40},{28,44},{32,4... | collective-permute-start | bytes 294920 | tf_op jit(solution)/shard_map/ppermute | solution.py:35
  28.9 9.8 %collective-permute-start.8 = (bf16[64,768]{1,0:T(8,128)(2,1)S(1)}, bf16[64,768]{1,0:T(8,128)(2,1)S(1)}, u32[]{:S(2)}, u32[]{:S(2)}) collective-permute-start(bf16[64,768]{1,0:T(8,128)(2,1)S(1)} %pad_maximum_fusion.1.refs_4_.refs_3_), channel_id=1, source_target_pairs={{0,48},{4,52},{8,56},{12,60},{16,0},{20,4},{24,8},{28,12},{32,16},... | collective-permute-start | bytes 294920 | tf_op jit(solution)/shard_map/ppermute | solution.py:35
  31.2 7.5 %collective-permute-start.5 = (bf16[64,768]{1,0:T(8,128)(2,1)S(1)}, bf16[64,768]{1,0:T(8,128)(2,1)S(1)}, u32[]{:S(2)}, u32[]{:S(2)}) collective-permute-start(bf16[64,768]{1,0:T(8,128)(2,1)S(1)} %pad_maximum_fusion.1.refs_4_.refs_3_), channel_id=1, source_target_pairs={{0,8},{4,12},{8,16},{12,20},{16,24},{20,28},{24,32},{28,36},{32,40... | collective-permute-start | bytes 294920 | tf_op jit(solution)/shard_map/ppermute | solution.py:35
  33.2 6.3 %collective-permute-start.6 = (bf16[64,768]{1,0:T(8,128)(2,1)S(1)}, bf16[64,768]{1,0:T(8,128)(2,1)S(1)}, u32[]{:S(2)}, u32[]{:S(2)}) collective-permute-start(bf16[64,768]{1,0:T(8,128)(2,1)S(1)} %pad_maximum_fusion.1.refs_4_.refs_3_), channel_id=1, source_target_pairs={{0,56},{4,60},{8,0},{12,4},{16,8},{20,12},{24,16},{28,20},{32,24},... | collective-permute-start | bytes 294920 | tf_op jit(solution)/shard_map/ppermute | solution.py:35
  36.7 10.4 %collective-permute-start.22 = (bf16[48,3456]{1,0:T(8,128)(2,1)S(1)}, bf16[48,3456]{1,0:T(8,128)(2,1)S(1)}, u32[]{:S(2)}, u32[]{:S(2)}) collective-permute-start(bf16[48,3456]{1,0:T(8,128)(2,1)S(1)} %constant_dynamic-update-slice_fusion.4.refs_13_), channel_id=1, source_target_pairs={{0,192},{4,196},{8,200},{12,204},{16,208},{20,212},{24,216},{28,22... | collective-permute-start | bytes 995336 | tf_op jit(solution)/shard_map/ppermute | solution.py:35
  38.7 6.9 %collective-permute-start.11 = (bf16[64,768]{1,0:T(8,128)(2,1)S(1)}, bf16[64,768]{1,0:T(8,128)(2,1)S(1)}, u32[]{:S(2)}, u32[]{:S(2)}) collective-permute-start(bf16[64,768]{1,0:T(8,128)(2,1)S(1)} %collective-permute-done.7.refs_7_.refs_6_), channel_id=1, source_target_pairs={{0,16},{4,20},{8,24},{12,28},{16,32},{20,36},{24,40},{28,44},{32,4... | collective-permute-start | bytes 294920 | tf_op jit(solution)/shard_map/ppermute | solution.py:35
  38.7 6.9 %collective-permute-start.9 = (bf16[64,768]{1,0:T(8,128)(2,1)S(1)}, bf16[64,768]{1,0:T(8,128)(2,1)S(1)}, u32[]{:S(2)}, u32[]{:S(2)}) collective-permute-start(bf16[64,768]{1,0:T(8,128)(2,1)S(1)} %collective-permute-done.7.refs_7_.refs_6_), channel_id=1, source_target_pairs={{0,8},{4,12},{8,16},{12,20},{16,24},{20,28},{24,32},{28,36},{32,40... | collective-permute-start | bytes 294920 | tf_op jit(solution)/shard_map/ppermute | solution.py:35
  39.5 12.8 %collective-permute-start.16 = (bf16[64,3456]{1,0:T(8,128)(2,1)S(1)}, bf16[64,3456]{1,0:T(8,128)(2,1)S(1)}, u32[]{:S(2)}, u32[]{:S(2)}) collective-permute-start(bf16[64,3456]{1,0:T(8,128)(2,1)S(1)} %constant_dynamic-update-slice_fusion.refs_12_), channel_id=1, source_target_pairs={{0,64},{4,68},{8,72},{12,76},{16,80},{20,84},{24,88},{28,92},{32,9... | collective-permute-start | bytes 1327112 | tf_op jit(solution)/shard_map/ppermute | solution.py:35
  45.7 8.9 %collective-permute-start.21 = (bf16[64,3456]{1,0:T(8,128)(2,1)S(1)}, bf16[64,3456]{1,0:T(8,128)(2,1)S(1)}, u32[]{:S(2)}, u32[]{:S(2)}) collective-permute-start(bf16[64,3456]{1,0:T(8,128)(2,1)S(1)} %constant_dynamic-update-slice_fusion.refs_12_), channel_id=1, source_target_pairs={{0,192},{4,196},{8,200},{12,204},{16,208},{20,212},{24,216},{28,22... | collective-permute-start | bytes 1327112 | tf_op jit(solution)/shard_map/ppermute | solution.py:35
  45.7 11.0 %collective-permute-start.20 = (bf16[48,3456]{1,0:T(8,128)(2,1)S(1)}, bf16[48,3456]{1,0:T(8,128)(2,1)S(1)}, u32[]{:S(2)}, u32[]{:S(2)}) collective-permute-start(bf16[48,3456]{1,0:T(8,128)(2,1)S(1)} %constant_dynamic-update-slice_fusion.4.refs_13_), channel_id=1, source_target_pairs={{0,64},{4,68},{8,72},{12,76},{16,80},{20,84},{24,88},{28,92},{32,9... | collective-permute-start | bytes 995336 | tf_op jit(solution)/shard_map/ppermute | solution.py:35
  47.1 3.8 %collective-permute-start.10 = (bf16[64,768]{1,0:T(8,128)(2,1)S(1)}, bf16[64,768]{1,0:T(8,128)(2,1)S(1)}, u32[]{:S(2)}, u32[]{:S(2)}) collective-permute-start(bf16[64,768]{1,0:T(8,128)(2,1)S(1)} %collective-permute-done.8.refs_8_.refs_7_), channel_id=1, source_target_pairs={{0,56},{4,60},{8,0},{12,4},{16,8},{20,12},{24,16},{28,20},{32,24},... | collective-permute-start | bytes 294920 | tf_op jit(solution)/shard_map/ppermute | solution.py:35
  50.9 17.1 %collective-permute-start.24 = (bf16[64,3456]{1,0:T(8,128)(2,1)S(1)}, bf16[64,3456]{1,0:T(8,128)(2,1)S(1)}, u32[]{:S(2)}, u32[]{:S(2)}) collective-permute-start(bf16[64,3456]{1,0:T(8,128)(2,1)S(1)} %pad_maximum_fusion), channel_id=1, source_target_pairs={{0,192},{4,196},{8,200},{12,204},{16,208},{20,212},{24,216},{28,22... | collective-permute-start | bytes 1327112 | tf_op jit(solution)/shard_map/ppermute | solution.py:35
  52.4 15.6 %collective-permute-start.23 = (bf16[64,3456]{1,0:T(8,128)(2,1)S(1)}, bf16[64,3456]{1,0:T(8,128)(2,1)S(1)}, u32[]{:S(2)}, u32[]{:S(2)}) collective-permute-start(bf16[64,3456]{1,0:T(8,128)(2,1)S(1)} %collective-permute-done.16.refs_13_), channel_id=1, source_target_pairs={{0,64},{4,68},{8,72},{12,76},{16,80},{20,84},{24,88},{28,92},{32,9... | collective-permute-start | bytes 1327112 | tf_op jit(solution)/shard_map/ppermute | solution.py:35
  74.2 15.1 %all-to-all-start = ((f32[32,8,128]{2,1,0:T(8,128)}), f32[32,8,128]{2,1,0:T(8,128)S(1)}, u32[]{:S(2)}, u32[]{:S(2)}) async-start(f32[32,8,128]{2,1,0:T(8,128)} %shard_map.61), calls=%async_computation | async-start | bytes 262144 | tf_op jit(solution)/shard_map/all_to_all | solution.py:277
  90.0 19.4 %all-to-all-start.1 = ((f32[8,1,128]{2,1,0:T(1,128)}), f32[8,1,128]{2,1,0:T(1,128)S(1)}, u32[]{:S(2)}, u32[]{:S(2)}) async-start(f32[8,1,128]{2,1,0:T(1,128)} %get-tuple-element.19), calls=%async_computation.1 | async-start | bytes 8192 | tf_op jit(solution)/shard_map/all_to_all | solution.py:287
